TPU v7x, 32 devices: a whole 2x2x4 slice. The times are simulated.
32 devices in a mesh: dp: 4 (over x, core), expert: 8 (over z, y).
Axes of the slice: x: 2, y: 2, z: 4, core: 2. Of those that a mesh axis runs over, the one named last changes fastest.
Arguments:
- queries: bfloat16 [2, 4, 8, 2048], P(None, 'dp', 'expert'), may hold values from -5 to 5
- cache_keys: bfloat16 [4, 8, 512, 512], P('dp', 'expert'), may hold values from -5 to 5
- cache_values: bfloat16 [4, 8, 512, 512], P('dp', 'expert'), may hold values from -6 to 6
- new_keys: bfloat16 [2, 4, 8, 512], P(None, 'dp', 'expert'), may hold values from -9 to 9
- new_values: bfloat16 [2, 4, 8, 512], P(None, 'dp', 'expert'), may hold values from -6 to 6
- cache_len: int32 [4, 8], P('dp', 'expert'), may hold values from 256 to 510, as said below
- o_proj: bfloat16 [2048, 4096], P(None, 'expert'), may hold values from -0.125 to 0.125
- residual_in: bfloat16 [2, 4, 8, 4096], P(None, 'dp', None, 'expert'), may hold values from -36 to 36
- norm_gain: float32 [4096], P('expert'), may hold values from 0.1 to 1.9
- router: float32 [4096, 8], P('expert'), may hold values from -0.09375 to 0.09375
- expert_gate: bfloat16 [8, 4096, 14336], P('expert', None, 'dp'), may hold values from -0.09375 to 0.09375
- expert_up: bfloat16 [8, 4096, 14336], P('expert', None, 'dp'), may hold values from -0.09375 to 0.09375
- expert_down: bfloat16 [8, 14336, 4096], P('expert', 'dp'), may hold values from -0.046875 to 0.046875
- routes: int32 [2, 4, 8, 2], replicated, may hold values from 0 to 7, all different within a row; in each aligned block of 8 rows (0 to 7, 8 to 15, ..., all dimensions but the last counted through in order) at most 4 rows name the same one
- answers: int32 [2, 4, 8], P(None, 'dp', 'expert'), may hold values from 0 to 127
- stop_mask: int32 [2, 4], P(None, 'dp'), may hold values 0 or 1
Outputs:
- residual_out: bfloat16 [2, 4, 8, 4096], P(None, 'dp', None, 'expert')
- vote_share: float32 [2, 4, 128], P(None, 'dp')
Inputs may be any that keep to these rules, and one draw needn't show every extreme that they name: `cache_len`: some sequence uses exactly 510 cached positions. `routes`: each token names 2 different experts; in each step, the tokens of the 1 prompts of one index of dp (all their samples together) name one expert at most 4 times.
All inputs are finite; a program needn't handle non-finite values. No bound on the sum of `stop_mask` on one device may be relied on, other than what follows from the above.
Results may differ from a plain program's by a relative error of at most 0.0055.
Values may be sent and summed in bfloat16 or wider, within the bound.
No kernel may reach another device: no remote copies, remote signals or barrier semaphores. Data moves between devices by JAX's collectives and lax.ppermute only.
A program may use at most 192 MiB of HBM per device.

v0:
```python
import jax
import jax.numpy as jnp
from jax import lax
from jax.sharding import PartitionSpec as P

D = 4096
E = 8
TOP = 2
HD = 128
QH = 16
KVH = 4
STEPS = 2
ANSWERS = 128
EPSILON = 1e-05


def attend(query, keys, values, fresh_keys, fresh_values, lengths):
    step_count = query.shape[0]
    row_count = query.shape[1]
    cache_size = keys.shape[1]
    group_size = QH // KVH
    score_scale = HD ** (-0.5)
    queried = query.reshape(step_count, row_count, KVH, group_size, HD)
    old_keys = keys.reshape(row_count, cache_size, KVH, HD)
    old_values = values.reshape(row_count, cache_size, KVH, HD)
    young_keys = fresh_keys.reshape(step_count, row_count, KVH, HD)
    young_values = fresh_values.reshape(step_count, row_count, KVH, HD)
    old_scores = (
        jnp.einsum("trkgd,rckd->rkgtc", queried, old_keys, preferred_element_type=jnp.float32)
        * score_scale
    )
    new_scores = (
        jnp.einsum("trkgd,urkd->rkgtu", queried, young_keys, preferred_element_type=jnp.float32)
        * score_scale
    )
    old_valid = jnp.arange(cache_size, dtype=jnp.int32)[None, :] < lengths[:, None]
    old_scores = jnp.where(old_valid[:, None, None, None, :], old_scores, -jnp.inf)
    new_valid = jnp.arange(step_count)[None, :] <= jnp.arange(step_count)[:, None]
    new_scores = jnp.where(new_valid, new_scores, -jnp.inf)
    highest = jnp.maximum(jnp.max(old_scores, -1), jnp.max(new_scores, -1))[..., None]
    old_exp = jnp.exp(old_scores - highest)
    new_exp = jnp.exp(new_scores - highest)
    denominator = jnp.sum(old_exp, -1, keepdims=True) + jnp.sum(new_exp, -1, keepdims=True)
    old_weights = (old_exp / denominator).astype(jnp.bfloat16)
    new_weights = (new_exp / denominator).astype(jnp.bfloat16)
    combined = jnp.einsum(
        "rkgtc,rckd->trkgd", old_weights, old_values, preferred_element_type=jnp.float32
    )
    combined = combined + jnp.einsum(
        "rkgtu,urkd->trkgd", new_weights, young_values, preferred_element_type=jnp.float32
    )
    return combined.reshape(step_count, row_count, QH * HD).astype(jnp.bfloat16)


def slot_tables(picks, capacity):
    block_count = picks.shape[0]
    row_count = picks.shape[1]
    expert_hot = (picks[..., None] == jnp.arange(E, dtype=jnp.int32)).astype(jnp.int32)
    expert_hot = expert_hot.reshape(block_count, row_count * TOP, E)
    earlier = jnp.cumsum(expert_hot, 1) - expert_hot
    place = jnp.sum(earlier * expert_hot, -1).reshape(block_count, row_count, TOP)
    slot_ids = picks * capacity + place
    return (slot_ids[..., None] == jnp.arange(E * capacity, dtype=jnp.int32)).astype(jnp.float32)


def on_device(
    queries,
    cache_keys,
    cache_values,
    new_keys,
    new_values,
    cache_len,
    o_proj,
    residual_in,
    norm_gain,
    router,
    expert_gate,
    expert_up,
    expert_down,
    routes,
    answers,
    stop_mask,
):
    prompt_dev = residual_in.shape[1]
    samples = residual_in.shape[2]
    columns = residual_in.shape[3]
    local_count = queries.shape[2]
    seq_count = prompt_dev * local_count
    cache_size = cache_keys.shape[2]
    spread = lax.axis_size("expert") // E
    capacity = 2 * prompt_dev * samples * TOP // E
    block_rows = prompt_dev * samples
    dp_index = lax.axis_index("dp")
    attended = attend(
        queries.reshape(STEPS, seq_count, QH * HD),
        cache_keys.reshape(seq_count, cache_size, KVH * HD),
        cache_values.reshape(seq_count, cache_size, KVH * HD),
        new_keys.reshape(STEPS, seq_count, KVH * HD),
        new_values.reshape(STEPS, seq_count, KVH * HD),
        cache_len.reshape(seq_count),
    ).reshape(STEPS, prompt_dev, local_count, QH * HD)
    active = (1 - stop_mask).astype(jnp.float32)
    attn_proj = jnp.einsum(
        "tpsq,qc->tpsc",
        lax.all_gather(attended, "expert", axis=2, tiled=True),
        o_proj,
        preferred_element_type=jnp.float32,
    )
    mixed_rows = residual_in.astype(jnp.float32) + attn_proj
    squares = jnp.sum(mixed_rows * mixed_rows, -1)
    scaled = mixed_rows * norm_gain
    squares_all = lax.psum(squares, "expert")
    inv_rms = lax.rsqrt(squares_all / D + EPSILON)[..., None]
    normed_f = scaled * inv_rms
    partial_logits = jnp.einsum("tpsc,ce->tpse", normed_f, router, precision=lax.Precision.HIGHEST)
    logits = lax.psum(partial_logits, "expert")
    normed = normed_f.astype(jnp.bfloat16)
    own_picks = lax.dynamic_slice_in_dim(routes, dp_index * prompt_dev, prompt_dev, 1)
    expert_hot = (own_picks[..., None] == jnp.arange(E, dtype=jnp.int32)).astype(jnp.float32)
    chosen = jnp.sum(expert_hot * logits[:, :, :, None, :], -1)
    gate_weights = jax.nn.sigmoid(chosen - chosen[..., ::-1]).reshape(STEPS, block_rows, TOP)
    own_table = slot_tables(own_picks.reshape(STEPS, block_rows, TOP), capacity)
    senders = jnp.sum(own_table, 2).astype(jnp.bfloat16)
    outgoing = jnp.einsum(
        "trs,trx->tsx",
        senders,
        normed.reshape(STEPS, block_rows, columns),
        preferred_element_type=jnp.float32,
    ).astype(jnp.bfloat16)
    outgoing = jnp.transpose(outgoing.reshape(STEPS, E, capacity, columns), (1, 0, 2, 3)).reshape(
        E, 1, STEPS * capacity, columns
    )
    outgoing = jnp.broadcast_to(outgoing, (E, spread, STEPS * capacity, columns)).reshape(
        E * spread, STEPS * capacity, columns
    )
    tokens = lax.all_gather(
        lax.all_to_all(outgoing, "expert", split_axis=0, concat_axis=2, tiled=True),
        "dp",
        axis=0,
        tiled=True,
    )
    gate_part = jnp.einsum(
        "...d,df->...f", tokens, expert_gate[0], preferred_element_type=jnp.float32
    )
    up_part = jnp.einsum("...d,df->...f", tokens, expert_up[0], preferred_element_type=jnp.float32)
    hidden = (jax.nn.silu(gate_part) * up_part).astype(jnp.bfloat16)
    partial_out = lax.psum_scatter(
        jnp.einsum("...f,fd->...d", hidden, expert_down[0], preferred_element_type=jnp.float32),
        "dp",
        scatter_dimension=0,
        tiled=True,
    )
    returned = lax.all_to_all(partial_out, "expert", split_axis=2, concat_axis=0, tiled=True)
    slot_out = jnp.sum(returned.reshape(E, spread, STEPS, capacity, columns), 1)
    slot_out = jnp.transpose(slot_out, (1, 0, 2, 3)).reshape(STEPS, E * capacity, columns)
    combine = jnp.einsum("trk,trks->trs", gate_weights, own_table)
    moe = jnp.einsum("trs,tsx->trx", combine, slot_out, precision=lax.Precision.HIGHEST).reshape(
        STEPS, prompt_dev, samples, columns
    )
    updated = residual_in.astype(jnp.float32) + active[:, :, None, None] * (attn_proj + moe)
    hits = jnp.sum(
        (answers[..., None] == jnp.arange(ANSWERS, dtype=jnp.int32)).astype(jnp.float32), 2
    )
    votes = active[:, :, None] * hits
    tallied = lax.psum(votes, "expert")
    running = jnp.cumsum(tallied, 0)
    shares = running / jnp.maximum(jnp.sum(running, -1, keepdims=True), 1.0)
    return (updated.astype(jnp.bfloat16), shares)


def solution(mesh):
    placed = (
        P(None, "dp", "expert", None),
        P("dp", "expert", None, None),
        P("dp", "expert", None, None),
        P(None, "dp", "expert", None),
        P(None, "dp", "expert", None),
        P("dp", "expert"),
        P(None, "expert"),
        P(None, "dp", None, "expert"),
        P("expert"),
        P("expert", None),
        P("expert", None, "dp"),
        P("expert", None, "dp"),
        P("expert", "dp", None),
        P(),
        P(None, "dp", "expert"),
        P(None, "dp"),
    )
    return jax.shard_map(
        on_device,
        mesh=mesh,
        in_specs=placed,
        out_specs=(P(None, "dp", None, "expert"), P(None, "dp", None)),
        check_vma=False,
    )
```

profile of v0, /device:TPU:0, one launch (start us, length us, event | category | flops | bytes accessed | tf_op | source)
XLA Modules:
  0.0 199.6 jit_solution(14043567168421434307)
XLA Ops:
  7.2 0.9 reshape.296
  8.1 1.2 reshape.295
  9.9 0.9 convolution_multiply_fusion.1
  11.6 1.2 reshape.299
  13.0 0.9 fusion.25
  13.9 32.4 %all_gather.6 = bf16[2,1,8,2048]{3,0,1,2:T(2,128)(2,1)S(1)} all-gather(bf16[2,1,1,2048]{3,0,1,2:T(2,128)(2,1)S(1)} %bitcast.171), channel_id=1, replica_groups=mesh['dp'=4,'expert'=8] {'expert'}, dimensions={2}, use_global_device_ids=true | all-gather | bytes 73728 | tf_op jit(solution)/shard_map/all_gather | solution.py:105
  46.3 1.2 multiply_reduce_fusion
  47.4 21.3 %psum.21 = f32[2,1,8]{2,0,1:T(2,128)S(1)} all-reduce(f32[2,1,8]{2,0,1:T(2,128)S(1)} %bitcast.173), channel_id=1, replica_groups=mesh['dp'=4,'expert'=8] {'expert'}, use_global_device_ids=true, to_apply=%region_5.6 | all-reduce | flops 16 | bytes 128 | tf_op jit(solution)/shard_map/psum | solution.py:112
  68.8 0.7 constant_dynamic-slice_fusion
  70.1 0.7 multiply_add_fusion
  70.9 0.9 convolution_convert_fusion
  71.9 0.6 copy.113
  72.5 3.3 %all-to-all-start = ((bf16[8,8,512]{2,1,0:T(8,128)(2,1)}), bf16[8,8,512]{2,1,0:T(8,128)(2,1)S(1)}, u32[]{:S(2)}, u32[]{:S(2)}) async-start(bf16[8,8,512]{2,1,0:T(8,128)(2,1)} %copy.113), calls=%async_computation | async-start | bytes 131072 | tf_op jit(solution)/shard_map/all_to_all | solution.py:137
  75.9 1.0 fusion.38
  76.9 0.7 convert_bitcast_fusion
  77.6 0.7 compare_select_fusion
  78.3 4.4 %all-to-all-done = bf16[8,8,512]{2,1,0:T(8,128)(2,1)S(1)} async-done(((bf16[8,8,512]{2,1,0:T(8,128)(2,1)}), bf16[8,8,512]{2,1,0:T(8,128)(2,1)S(1)}, u32[]{:S(2)}, u32[]{:S(2)}) %all-to-all-start) | async-done | bytes 65568 | tf_op jit(solution)/shard_map/all_to_all | solution.py:137
  82.7 5.8 %all_gather.7 = bf16[4,8,4096]{2,1,0:T(8,128)(2,1)S(1)} all-gather(bf16[1,8,4096]{2,1,0:T(8,128)(2,1)S(1)} %bitcast.169), channel_id=1, replica_groups=mesh['dp'=4,'expert'=8] {'dp'}, dimensions={0}, use_global_device_ids=true | all-gather | bytes 327680 | tf_op jit(solution)/shard_map/all_gather | solution.py:136
  88.5 11.8 %fusion.4 = f32[4,8,3584]{2,1,0:T(8,128)S(1)} fusion(bf16[4,8,4096]{2,1,0:T(8,128)(2,1)S(1)} %all_gather.7, bf16[1,4096,3584]{2,1,0:T(8,128)(2,1)} %param.26), kind=kOutput, calls=%fused_computation.4 | convolution fusion | flops 939524096 | bytes 30081024 | tf_op jit(solution)/shard_map/...d,df->...f/dot_general | solution.py:142
  100.3 22.4 %fusion = f32[4,8,4096]{2,1,0:T(8,128)} fusion(bf16[1,3584,4096]{2,1,0:T(8,128)(2,1)} %param.28, bf16[4,8,4096]{2,1,0:T(8,128)(2,1)S(1)} %all_gather.7, bf16[1,4096,3584]{2,1,0:T(8,128)(2,1)} %param.27, f32[4,8,3584]{2,1,0:T(8,128)S(1)} %fusion.4), kind=kOutput, calls=%fused_computation | convolution fusion | flops 1879736320 | bytes 59965440 | tf_op jit(solution)/shard_map/...f,fd->...d/dot_general | solution.py:148
  122.7 0.7 fusion.72
  123.4 18.6 %all-reduce = (f32[2,8,8]{2,1,0:T(8,128)S(1)}, f32[2,1,128]{2,1,0:T(1,128)S(1)}) all-reduce(f32[2,8,8]{2,1,0:T(8,128)S(1)} %fusion.38, f32[2,1,128]{2,1,0:T(1,128)S(1)} %compare_select_fusion), channel_id=1, replica_groups=mesh['dp'=4,'expert'=8] {'expert'}, use_global_device_ids=true, to_apply=%region_6.7 | all-reduce | flops 384 | bytes 3072 | tf_op jit(solution)/shard_map/psum | solution.py:116
  142.4 4.8 %copy.114 = f32[1,8,4096]{1,0,2:T(1,128)} copy(f32[1,8,4096]{2,1,0:T(8,128)} %reduce-scatter.2.cloned.1.call-done) | data formatting | bytes 262144 | tf_op jit(solution)/shard_map/reduce_scatter | solution.py:147
  147.7 20.4 %reduce.7 = f32[4096,8]{1,0:T(8,128)} reduce(f32[4096,1,8]{2,1,0:T(1,128)} %bitcast.164, f32[]{:T(128)} %broadcast.178), dimensions={1}, to_apply=%bitcast.149.reduce_sub_computation | reduce | bytes 262148
  168.0 3.3 %reshape.320 = f32[8,1,4096]{2,1,0:T(1,128)} reshape(f32[4096,8]{1,0:T(8,128)} %reduce.7) | data formatting | bytes 262144
  171.3 5.1 %all-to-all-start.1 = ((f32[8,1,4096]{2,1,0:T(1,128)}), f32[8,1,4096]{2,1,0:T(1,128)S(1)}, u32[]{:S(2)}, u32[]{:S(2)}) async-start(f32[8,1,4096]{2,1,0:T(1,128)} %reshape.320), calls=%async_computation.2 | async-start | bytes 262144 | tf_op jit(solution)/shard_map/all_to_all | solution.py:153
  176.5 0.6 broadcast_divide_fusion
  177.4 6.5 %all-to-all-done.1 = f32[8,1,4096]{2,1,0:T(1,128)S(1)} async-done(((f32[8,1,4096]{2,1,0:T(1,128)}), f32[8,1,4096]{2,1,0:T(1,128)S(1)}, u32[]{:S(2)}, u32[]{:S(2)}) %all-to-all-start.1) | async-done | bytes 131104 | tf_op jit(solution)/shard_map/all_to_all | solution.py:153
  183.8 1.0 reduce.8
  184.8 4.9 %reshape.321 = f32[4096,1,8]{2,1,0:T(1,128)} reshape(f32[8,4096]{1,0:T(8,128)S(1)} %reduce.8) | data formatting | bytes 262144
  189.6 2.2 %copy.131 = f32[1,8,8,512]{3,2,1,0:T(8,128)S(1)} copy(f32[1,8,8,512]{1,3,2,0:T(8,128)} %bitcast.165) | data formatting | bytes 262144 | tf_op jit(solution)/shard_map/all_to_all | solution.py:153
  192.0 0.8 fusion.23
  (42 shorter events, 3.2 us)
Async XLA Ops:
  7.2 39.1 %copy-start = (bf16[2048,512]{1,0:T(8,128)(2,1)S(1)}, bf16[2048,512]{1,0:T(8,128)(2,1)}, u32[]{:S(2)}) copy-start(bf16[2048,512]{1,0:T(8,128)(2,1)} %param.22) | copy-start | bytes 6291460
  72.5 10.2 %all-to-all-start = ((bf16[8,8,512]{2,1,0:T(8,128)(2,1)}), bf16[8,8,512]{2,1,0:T(8,128)(2,1)S(1)}, u32[]{:S(2)}, u32[]{:S(2)}) async-start(bf16[8,8,512]{2,1,0:T(8,128)(2,1)} %copy.113), calls=%async_computation | async-start | bytes 131072 | tf_op jit(solution)/shard_map/all_to_all | solution.py:137
  75.9 66.5 %reduce-scatter.2.cloned.1.call-start = ((), (), s32[]{:S(2)}) async-start(), calls=%async_computation.3 | async-start | bytes 655360 | tf_op jit(solution)/shard_map/reduce_scatter | solution.py:147
  100.3 91.7 %copy-start.1 = (bf16[2,1,8,512]{3,2,1,0:T(8,128)(2,1)S(1)}, bf16[2,1,8,512]{3,2,1,0:T(8,128)(2,1)}, u32[]{:S(2)}) copy-start(bf16[2,1,8,512]{3,2,1,0:T(8,128)(2,1)} %param.23) | copy-start | bytes 49156
  171.3 12.5 %all-to-all-start.1 = ((f32[8,1,4096]{2,1,0:T(1,128)}), f32[8,1,4096]{2,1,0:T(1,128)S(1)}, u32[]{:S(2)}, u32[]{:S(2)}) async-start(f32[8,1,4096]{2,1,0:T(1,128)} %reshape.320), calls=%async_computation.2 | async-start | bytes 262144 | tf_op jit(solution)/shard_map/all_to_all | solution.py:153
Sparse Core Ops, SparseCore 0:
  122.9 19.1 reduce-scatter.1
where the time goes:
time: 201 us; the launch traced here: 200 us
  blocking collectives  78 us (39%)
  matrix products  40.6 us (20%)
  other arithmetic  25.3 us (13%)
  local copies, waits for them, and re-layouts  21.5 us (11%)
  between operations  14.8 us (7%)
  waiting for transfers between devices  10.9 us (5%)
  starting transfers between devices  8.52 us (4%)
    all_gather x1, blocking collectives, on_device(): lax.all_gather(attended, 'expert', axis=2, tiled=True)  32.4 us
    dot_general x1, matrix products, on_device(): jnp.einsum('...f,fd->...d', hidden, expert_down[0], preferred_element_typ...  22.4 us
    psum x1, blocking collectives, on_device(): squares_all = lax.psum(squares, 'expert')  21.3 us
    unnamed x1, other arithmetic  20.4 us
    psum x1, blocking collectives, on_device(): logits = lax.psum(partial_logits, 'expert')  18.6 us
    dot_general x1, matrix products, on_device(): jnp.einsum('...d,df->...f', tokens, expert_gate[0], preferred_element_typ...  11.8 us
    unnamed x7, local copies, waits for them, and re-layouts  8.7 us
    all_to_all x1, waiting for transfers between devices, on_device(): lax.all_to_all(partial_out, 'expert', split_axis=2, concat_axis=0, tiled=...  6.46 us
  transfers between devices with their start and end apart: 3, of which 2 were waited for; matrix products, arithmetic and copies ran while one was open for 2% of the time, Pallas kernels for 0%

commit v1 on v0

--- a/solution.py
+++ b/solution.py
@@ -100,11 +100,54 @@
         cache_len.reshape(seq_count),
     ).reshape(STEPS, prompt_dev, local_count, QH * HD)
     active = (1 - stop_mask).astype(jnp.float32)
-    attn_proj = jnp.einsum(
-        "tpsq,qc->tpsc",
-        lax.all_gather(attended, "expert", axis=2, tiled=True),
-        o_proj,
-        preferred_element_type=jnp.float32,
+
+    def _move_cubes(obj, arr_in):
+        all_rows, part_next, a_next = (
+            lax.axis_size("expert"),
+            lax.axis_index("expert"),
+            obj.shape[2],
+        )
+        found = tuple(((nth, (nth + 1) % all_rows) for nth in range(all_rows)))
+        row_list = tuple(((dev_i, j0) for j0, dev_i in found))
+        r2, w1 = (
+            lax.ppermute(obj, "expert", perm=found),
+            lax.ppermute(obj, "expert", perm=row_list),
+        )
+        current_block = arr_in(obj, part_next * a_next)
+        h_now = current_block.shape[2]
+        current_value = jnp.zeros(
+            (*current_block.shape[:2], all_rows * h_now, *current_block.shape[3:]),
+            current_block.dtype,
+        )
+
+        def play_widths(current_value, current_block, vec_out):
+            return lax.dynamic_update_slice_in_dim(
+                current_value, current_block, vec_out * h_now, axis=2
+            )
+
+        current_value = play_widths(current_value, current_block, part_next)
+        d = 1
+        while d < all_rows // 2 + 1:
+            n_now, latest = ((part_next - d) % all_rows, (part_next + d) % all_rows)
+            q_next = (r2, w1)
+            if d < all_rows // 2:
+                r2, w1 = (
+                    lax.ppermute(r2, "expert", perm=found),
+                    lax.ppermute(w1, axis_name="expert", perm=row_list),
+                )
+            current_value = play_widths(current_value, arr_in(q_next[0], n_now * a_next), n_now)
+            if 2 * d < all_rows:
+                current_value = play_widths(
+                    current_value, arr_in(q_next[1], latest * a_next), latest
+                )
+            d += 1
+        return current_value
+
+    attn_proj = _move_cubes(
+        attended,
+        lambda shard, start: jnp.einsum(
+            "tpsq,qc->tpsc", shard, o_proj, preferred_element_type=jnp.float32
+        ),
     )
     mixed_rows = residual_in.astype(jnp.float32) + attn_proj
     squares = jnp.sum(mixed_rows * mixed_rows, -1)

time: 201 us -> 186 us (0.925)
  blocking collectives: 78 us -> 41.7 us
  starting transfers between devices: 8.52 us -> 24.9 us
  waiting for transfers between devices: 10.9 us -> 21.2 us
  other arithmetic: 25.3 us -> 22.5 us
  local copies, waits for them, and re-layouts: 21.5 us -> 19.2 us
    all_gather x1 -> x0, blocking collectives: 32.4 us -> none  [on_device(): lax.all_gather(attended, 'expert', axis=2, tiled=True)]
    ppermute x0 -> x7, starting transfers between devices: none -> 15.9 us  [the longest x2 9.76 us: _move_cubes(): lax.ppermute(w1, axis_name='expert', perm=row_list)]
    ppermute x0 -> x7, waiting for transfers between devices: none -> 7.74 us  [the longest x3 7.45 us: _move_cubes(): lax.ppermute(r2, 'expert', perm=found)]
    psum x1, blocking collectives: 21.3 us -> 17.1 us  [on_device(): squares_all = lax.psum(squares, 'expert')]
    all_to_all x1, waiting for transfers between devices: 4.42 us -> 6.71 us  [on_device(): lax.all_to_all(outgoing, 'expert', split_axis=0, concat_axis=2, tiled=True)]
    unnamed x7 -> x23, local copies, waits for them, and re-layouts: 8.7 us -> 8.75 us
  transfers between devices with their start and end apart: 3 -> 10, of which waited for: 2 -> 8; matrix products, arithmetic and copies ran while one was open for 2% -> 3% of each run, Pallas kernels for 0% -> 0%
where the time goes in v1:
time: 186 us; the launch traced here: 185 us
  blocking collectives  41.7 us (22%)
  matrix products  40.2 us (22%)
  starting transfers between devices  24.9 us (13%)
  other arithmetic  22.5 us (12%)
  waiting for transfers between devices  21.2 us (11%)
  local copies, waits for them, and re-layouts  19.2 us (10%)
  between operations  15.2 us (8%)
    dot_general x1, matrix products, on_device(): jnp.einsum('...f,fd->...d', hidden, expert_down[0], preferred_element_typ...  22.4 us
    unnamed x1, other arithmetic  19.4 us
    psum x1, blocking collectives, on_device(): logits = lax.psum(partial_logits, 'expert')  18.6 us
    psum x1, blocking collectives, on_device(): squares_all = lax.psum(squares, 'expert')  17.1 us
    dot_general x1, matrix products, on_device(): jnp.einsum('...d,df->...f', tokens, expert_gate[0], preferred_element_typ...  11.8 us
    ppermute x2, starting transfers between devices, _move_cubes(): lax.ppermute(w1, axis_name='expert', perm=row_list)  9.76 us
    unnamed x23, local copies, waits for them, and re-layouts  8.75 us
    ppermute x3, waiting for transfers between devices, _move_cubes(): lax.ppermute(r2, 'expert', perm=found)  7.45 us
  transfers between devices with their start and end apart: 10, of which 8 were waited for; matrix products, arithmetic and copies ran while one was open for 3% of the time, Pallas kernels for 0%

profile of v1, /device:TPU:0, one launch (start us, length us, event | category | flops | bytes accessed | tf_op | source)
XLA Modules:
  0.0 184.8 jit_solution(10619740759047205360)
XLA Ops:
  7.2 0.9 reshape.325
  8.1 1.2 reshape.324
  10.0 0.9 convolution_multiply_fusion.1
  12.3 3.0 %collective-permute-start = (bf16[2,1,1,2048]{3,0,2,1:T(2,128)(2,1)S(1)}, bf16[2,1,1,2048]{3,0,2,1:T(2,128)(2,1)S(1)}, u32[]{:S(2)}, u32[]{:S(2)}) collective-permute-start(bf16[2,1,1,2048]{3,0,2,1:T(2,128)(2,1)S(1)} %convert_element_type.81), channel_id=1, source_target_pairs={{0,1},{1,2},{2,3},{3,4},{4,5},{5,6},{6,7},{7,0},{8,9},{9,10},{10,1... | collective-permute-start | bytes 24584 | tf_op jit(solution)/shard_map/ppermute | solution.py:113
  15.3 3.1 %collective-permute-start.1 = (bf16[2,1,1,2048]{3,0,2,1:T(2,128)(2,1)S(1)}, bf16[2,1,1,2048]{3,0,2,1:T(2,128)(2,1)S(1)}, u32[]{:S(2)}, u32[]{:S(2)}) collective-permute-start(bf16[2,1,1,2048]{3,0,2,1:T(2,128)(2,1)S(1)} %convert_element_type.81), channel_id=1, source_target_pairs={{1,0},{2,1},{3,2},{4,3},{5,4},{6,5},{7,6},{0,7},{9,8},{10,9},{11,1... | collective-permute-start | bytes 24584 | tf_op jit(solution)/shard_map/ppermute | solution.py:114
  19.2 0.4 convolution_bitcast_fusion.8
  20.4 0.4 convolution_bitcast_fusion.6
  20.9 4.8 %collective-permute-start.3 = (bf16[2,1,1,2048]{3,0,2,1:T(2,128)(2,1)S(1)}, bf16[2,1,1,2048]{3,0,2,1:T(2,128)(2,1)S(1)}, u32[]{:S(2)}, u32[]{:S(2)}) collective-permute-start(bf16[2,1,1,2048]{3,0,2,1:T(2,128)(2,1)S(1)} %collective-permute-done.1), channel_id=1, source_target_pairs={{1,0},{2,1},{3,2},{4,3},{5,4},{6,5},{7,6},{0,7},{9,8},{10,9},{11,1... | collective-permute-start | bytes 24584 | tf_op jit(solution)/shard_map/ppermute | solution.py:136
  25.7 1.0 collective-permute-done.2
  27.1 0.4 convolution_bitcast_fusion.4
  27.7 5.0 %collective-permute-start.5 = (bf16[2,1,1,2048]{3,0,2,1:T(2,128)(2,1)S(1)}, bf16[2,1,1,2048]{3,0,2,1:T(2,128)(2,1)S(1)}, u32[]{:S(2)}, u32[]{:S(2)}) collective-permute-start(bf16[2,1,1,2048]{3,0,2,1:T(2,128)(2,1)S(1)} %collective-permute-done.3), channel_id=1, source_target_pairs={{1,0},{2,1},{3,2},{4,3},{5,4},{6,5},{7,6},{0,7},{9,8},{10,9},{11,1... | collective-permute-start | bytes 24584 | tf_op jit(solution)/shard_map/ppermute | solution.py:136
  32.7 0.8 collective-permute-done.4
  34.6 5.6 %collective-permute-done.6 = bf16[2,1,1,2048]{3,0,2,1:T(2,128)(2,1)S(1)} collective-permute-done((bf16[2,1,1,2048]{3,0,2,1:T(2,128)(2,1)S(1)}, bf16[2,1,1,2048]{3,0,2,1:T(2,128)(2,1)S(1)}, u32[]{:S(2)}, u32[]{:S(2)}) %collective-permute-start.6) | collective-permute-done | bytes 8224 | tf_op jit(solution)/shard_map/ppermute | solution.py:135
  40.7 17.1 %psum.21 = f32[2,1,8]{2,0,1:T(2,128)S(1)} all-reduce(f32[2,1,8]{2,0,1:T(2,128)S(1)} %bitcast.203), channel_id=1, replica_groups=mesh['dp'=4,'expert'=8] {'expert'}, use_global_device_ids=true, to_apply=%region_5.6 | all-reduce | flops 16 | bytes 128 | tf_op jit(solution)/shard_map/psum | solution.py:155
  58.1 0.6 copy.150
  58.8 3.3 %all-to-all-start = ((bf16[8,8,512]{2,1,0:T(8,128)(2,1)}), bf16[8,8,512]{2,1,0:T(8,128)(2,1)S(1)}, u32[]{:S(2)}, u32[]{:S(2)}) async-start(bf16[8,8,512]{2,1,0:T(8,128)(2,1)} %copy.150), calls=%async_computation | async-start | bytes 131072 | tf_op jit(solution)/shard_map/all_to_all | solution.py:180
  62.3 6.7 %all-to-all-done = bf16[8,8,512]{2,1,0:T(8,128)(2,1)S(1)} async-done(((bf16[8,8,512]{2,1,0:T(8,128)(2,1)}), bf16[8,8,512]{2,1,0:T(8,128)(2,1)S(1)}, u32[]{:S(2)}, u32[]{:S(2)}) %all-to-all-start) | async-done | bytes 65568 | tf_op jit(solution)/shard_map/all_to_all | solution.py:180
  69.0 6.0 %all_gather.3 = bf16[4,8,4096]{2,1,0:T(8,128)(2,1)S(1)} all-gather(bf16[1,8,4096]{2,1,0:T(8,128)(2,1)S(1)} %bitcast.200), channel_id=1, replica_groups=mesh['dp'=4,'expert'=8] {'dp'}, dimensions={0}, use_global_device_ids=true | all-gather | bytes 327680 | tf_op jit(solution)/shard_map/all_gather | solution.py:179
  74.9 11.8 %fusion.4 = f32[4,8,3584]{2,1,0:T(8,128)S(1)} fusion(bf16[4,8,4096]{2,1,0:T(8,128)(2,1)S(1)} %all_gather.3, bf16[1,4096,3584]{2,1,0:T(8,128)(2,1)} %param.26), kind=kOutput, calls=%fused_computation.4 | convolution fusion | flops 939524096 | bytes 30081024 | tf_op jit(solution)/shard_map/...d,df->...f/dot_general | solution.py:185
  86.7 22.4 %fusion = f32[4,8,4096]{2,1,0:T(8,128)} fusion(bf16[1,3584,4096]{2,1,0:T(8,128)(2,1)} %param.28, bf16[4,8,4096]{2,1,0:T(8,128)(2,1)S(1)} %all_gather.3, bf16[1,4096,3584]{2,1,0:T(8,128)(2,1)} %param.27, f32[4,8,3584]{2,1,0:T(8,128)S(1)} %fusion.4), kind=kOutput, calls=%fused_computation | convolution fusion | flops 1879736320 | bytes 59965440 | tf_op jit(solution)/shard_map/...f,fd->...d/dot_general | solution.py:191
  109.4 18.6 %all-reduce = (f32[2,8,8]{2,1,0:T(8,128)S(1)}, f32[2,1,128]{2,1,0:T(1,128)S(1)}) all-reduce(f32[2,8,8]{2,1,0:T(8,128)S(1)} %fusion.34, f32[2,1,128]{2,1,0:T(1,128)S(1)} %compare_select_fusion), channel_id=1, replica_groups=mesh['dp'=4,'expert'=8] {'expert'}, use_global_device_ids=true, to_apply=%region_6.7 | all-reduce | flops 384 | bytes 3072 | tf_op jit(solution)/shard_map/psum | solution.py:159
  128.6 4.1 %copy.151 = f32[1,8,4096]{1,0,2:T(1,128)S(1)} copy(f32[1,8,4096]{2,1,0:T(8,128)} %reduce-scatter.2.cloned.1.call-done) | data formatting | bytes 262144 | tf_op jit(solution)/shard_map/reduce_scatter | solution.py:190
  132.7 0.5 broadcast.184
  133.3 19.4 %reduce.7 = f32[4096,8]{1,0:T(8,128)} reduce(f32[4096,1,8]{2,1,0:T(1,128)S(1)} %bitcast.195, f32[]{:T(128)} %broadcast.184), dimensions={1}, to_apply=%bitcast.175.reduce_sub_computation | reduce | bytes 262148
  152.6 3.3 %reshape.355 = f32[8,1,4096]{2,1,0:T(1,128)} reshape(f32[4096,8]{1,0:T(8,128)} %reduce.7) | data formatting | bytes 262144
  156.0 5.6 %all-to-all-start.1 = ((f32[8,1,4096]{2,1,0:T(1,128)}), f32[8,1,4096]{2,1,0:T(1,128)S(1)}, u32[]{:S(2)}, u32[]{:S(2)}) async-start(f32[8,1,4096]{2,1,0:T(1,128)} %reshape.355), calls=%async_computation.2 | async-start | bytes 262144 | tf_op jit(solution)/shard_map/all_to_all | solution.py:196
  161.5 0.6 broadcast_divide_fusion
  162.4 6.5 %all-to-all-done.1 = f32[8,1,4096]{2,1,0:T(1,128)S(1)} async-done(((f32[8,1,4096]{2,1,0:T(1,128)}), f32[8,1,4096]{2,1,0:T(1,128)S(1)}, u32[]{:S(2)}, u32[]{:S(2)}) %all-to-all-start.1) | async-done | bytes 131104 | tf_op jit(solution)/shard_map/all_to_all | solution.py:196
  168.9 1.1 reduce.8
  170.0 4.9 %reshape.356 = f32[4096,1,8]{2,1,0:T(1,128)} reshape(f32[8,4096]{1,0:T(8,128)S(1)} %reduce.8) | data formatting | bytes 262144
  174.8 2.2 %copy.168 = f32[1,8,8,512]{3,2,1,0:T(8,128)S(1)} copy(f32[1,8,8,512]{1,3,2,0:T(8,128)} %bitcast.196) | data formatting | bytes 262144 | tf_op jit(solution)/shard_map/all_to_all | solution.py:196
  177.2 0.8 fusion.21
  (97 shorter events, 6.7 us)
Async XLA Ops:
  7.2 12.0 %copy-start = (bf16[2048,512]{1,0:T(8,128)(2,1)S(1)}, bf16[2048,512]{1,0:T(8,128)(2,1)}, u32[]{:S(2)}) copy-start(bf16[2048,512]{1,0:T(8,128)(2,1)} %param.22) | copy-start | bytes 6291460
  7.2 4.5 %copy-start.2 = (bf16[1,1,512,512]{3,2,1,0:T(8,128)(2,1)S(1)}, bf16[1,1,512,512]{3,2,1,0:T(8,128)(2,1)}, u32[]{:S(2)}) copy-start(bf16[1,1,512,512]{3,2,1,0:T(8,128)(2,1)} %param.18) | copy-start | bytes 1572868
  8.1 4.0 %copy-start.8 = (bf16[2,1,1,512]{3,0,2,1:T(2,128)(2,1)S(1)}, bf16[2,1,1,512]{3,0,2,1:T(2,128)(2,1)}, u32[]{:S(2)}) copy-start(bf16[2,1,1,512]{3,0,2,1:T(2,128)(2,1)} %param.20) | copy-start | bytes 6148
  8.1 10.4 %copy-start.6 = (s32[2,4,8,2]{2,3,1,0:T(2,128)S(1)}, s32[2,4,8,2]{2,3,1,0:T(2,128)}, u32[]{:S(2)}) copy-start(s32[2,4,8,2]{2,3,1,0:T(2,128)} %param.29) | copy-start | bytes 1540
  8.1 11.0 %copy-start.9 = (s32[2,1]{0,1:T(1,128)S(1)}, s32[2,1]{0,1:T(1,128)}, u32[]{:S(2)}) copy-start(s32[2,1]{0,1:T(1,128)} %param.31) | copy-start | bytes 28
  12.3 7.7 %collective-permute-start = (bf16[2,1,1,2048]{3,0,2,1:T(2,128)(2,1)S(1)}, bf16[2,1,1,2048]{3,0,2,1:T(2,128)(2,1)S(1)}, u32[]{:S(2)}, u32[]{:S(2)}) collective-permute-start(bf16[2,1,1,2048]{3,0,2,1:T(2,128)(2,1)S(1)} %convert_element_type.81), channel_id=1, source_target_pairs={{0,1},{1,2},{2,3},{3,4},{4,5},{5,6},{6,7},{7,0},{8,9},{9,10},{10,1... | collective-permute-start | bytes 24584 | tf_op jit(solution)/shard_map/ppermute | solution.py:113
  15.3 5.0 %collective-permute-start.1 = (bf16[2,1,1,2048]{3,0,2,1:T(2,128)(2,1)S(1)}, bf16[2,1,1,2048]{3,0,2,1:T(2,128)(2,1)S(1)}, u32[]{:S(2)}, u32[]{:S(2)}) collective-permute-start(bf16[2,1,1,2048]{3,0,2,1:T(2,128)(2,1)S(1)} %convert_element_type.81), channel_id=1, source_target_pairs={{1,0},{2,1},{3,2},{4,3},{5,4},{6,5},{7,6},{0,7},{9,8},{10,9},{11,1... | collective-permute-start | bytes 24584 | tf_op jit(solution)/shard_map/ppermute | solution.py:114
  20.4 6.4 %collective-permute-start.2 = (bf16[2,1,1,2048]{3,0,2,1:T(2,128)(2,1)S(1)}, bf16[2,1,1,2048]{3,0,2,1:T(2,128)(2,1)S(1)}, u32[]{:S(2)}, u32[]{:S(2)}) collective-permute-start(bf16[2,1,1,2048]{3,0,2,1:T(2,128)(2,1)S(1)} %collective-permute-done), channel_id=1, source_target_pairs={{0,1},{1,2},{2,3},{3,4},{4,5},{5,6},{6,7},{7,0},{8,9},{9,10},{10,1... | collective-permute-start | bytes 24584 | tf_op jit(solution)/shard_map/ppermute | solution.py:135
  20.9 6.2 %collective-permute-start.3 = (bf16[2,1,1,2048]{3,0,2,1:T(2,128)(2,1)S(1)}, bf16[2,1,1,2048]{3,0,2,1:T(2,128)(2,1)S(1)}, u32[]{:S(2)}, u32[]{:S(2)}) collective-permute-start(bf16[2,1,1,2048]{3,0,2,1:T(2,128)(2,1)S(1)} %collective-permute-done.1), channel_id=1, source_target_pairs={{1,0},{2,1},{3,2},{4,3},{5,4},{6,5},{7,6},{0,7},{9,8},{10,9},{11,1... | collective-permute-start | bytes 24584 | tf_op jit(solution)/shard_map/ppermute | solution.py:136
  27.1 6.4 %collective-permute-start.4 = (bf16[2,1,1,2048]{3,0,2,1:T(2,128)(2,1)S(1)}, bf16[2,1,1,2048]{3,0,2,1:T(2,128)(2,1)S(1)}, u32[]{:S(2)}, u32[]{:S(2)}) collective-permute-start(bf16[2,1,1,2048]{3,0,2,1:T(2,128)(2,1)S(1)} %collective-permute-done.2), channel_id=1, source_target_pairs={{0,1},{1,2},{2,3},{3,4},{4,5},{5,6},{6,7},{7,0},{8,9},{9,10},{10,1... | collective-permute-start | bytes 24584 | tf_op jit(solution)/shard_map/ppermute | solution.py:135
  27.7 6.4 %collective-permute-start.5 = (bf16[2,1,1,2048]{3,0,2,1:T(2,128)(2,1)S(1)}, bf16[2,1,1,2048]{3,0,2,1:T(2,128)(2,1)S(1)}, u32[]{:S(2)}, u32[]{:S(2)}) collective-permute-start(bf16[2,1,1,2048]{3,0,2,1:T(2,128)(2,1)S(1)} %collective-permute-done.3), channel_id=1, source_target_pairs={{1,0},{2,1},{3,2},{4,3},{5,4},{6,5},{7,6},{0,7},{9,8},{10,9},{11,1... | collective-permute-start | bytes 24584 | tf_op jit(solution)/shard_map/ppermute | solution.py:136
  33.8 6.8 %copy-start.3 = (bf16[2,1,8,512]{3,2,1,0:T(8,128)(2,1)S(1)}, bf16[2,1,8,512]{3,2,1,0:T(8,128)(2,1)}, u32[]{:S(2)}) copy-start(bf16[2,1,8,512]{3,2,1,0:T(8,128)(2,1)} %param.23) | copy-start | bytes 49156
  33.8 24.0 %copy-start.5 = (f32[512]{0:T(512)S(1)}, f32[512]{0:T(512)}, u32[]{:S(2)}) copy-start(f32[512]{0:T(512)} %param.24) | copy-start | bytes 6148
  33.8 28.4 %copy-start.7 = (s32[2,1,1]{0,2,1:T(1,128)S(1)}, s32[2,1,1]{0,2,1:T(1,128)}, u32[]{:S(2)}) copy-start(s32[2,1,1]{0,2,1:T(1,128)} %param.30) | copy-start | bytes 28
  33.8 6.4 %collective-permute-start.6 = (bf16[2,1,1,2048]{3,0,2,1:T(2,128)(2,1)S(1)}, bf16[2,1,1,2048]{3,0,2,1:T(2,128)(2,1)S(1)}, u32[]{:S(2)}, u32[]{:S(2)}) collective-permute-start(bf16[2,1,1,2048]{3,0,2,1:T(2,128)(2,1)S(1)} %collective-permute-done.4), channel_id=1, source_target_pairs={{0,1},{1,2},{2,3},{3,4},{4,5},{5,6},{6,7},{7,0},{8,9},{9,10},{10,1... | collective-permute-start | bytes 24584 | tf_op jit(solution)/shard_map/ppermute | solution.py:135
  58.8 10.2 %all-to-all-start = ((bf16[8,8,512]{2,1,0:T(8,128)(2,1)}), bf16[8,8,512]{2,1,0:T(8,128)(2,1)S(1)}, u32[]{:S(2)}, u32[]{:S(2)}) async-start(bf16[8,8,512]{2,1,0:T(8,128)(2,1)} %copy.150), calls=%async_computation | async-start | bytes 131072 | tf_op jit(solution)/shard_map/all_to_all | solution.py:180
  62.1 66.5 %reduce-scatter.2.cloned.1.call-start = ((), (), s32[]{:S(2)}) async-start(), calls=%async_computation.3 | async-start | bytes 655360 | tf_op jit(solution)/shard_map/reduce_scatter | solution.py:190
  86.7 22.5 %copy-start.4 = (f32[512,8]{0,1:T(8,128)S(1)}, f32[512,8]{0,1:T(8,128)}, u32[]{:S(2)}) copy-start(f32[512,8]{0,1:T(8,128)} %param.25) | copy-start | bytes 49156
  156.0 12.9 %all-to-all-start.1 = ((f32[8,1,4096]{2,1,0:T(1,128)}), f32[8,1,4096]{2,1,0:T(1,128)S(1)}, u32[]{:S(2)}, u32[]{:S(2)}) async-start(f32[8,1,4096]{2,1,0:T(1,128)} %reshape.355), calls=%async_computation.2 | async-start | bytes 262144 | tf_op jit(solution)/shard_map/all_to_all | solution.py:196
  168.9 9.1 %copy-start.1 = (bf16[2048,512]{1,0:T(8,128)(2,1)S(1)}, bf16[2048,512]{1,0:T(8,128)(2,1)}, u32[]{:S(2)}) copy-start(bf16[2048,512]{1,0:T(8,128)(2,1)} %param.22) | copy-start | bytes 6291460
Sparse Core Ops, SparseCore 0:
  109.3 19.2 reduce-scatter.1
